TPU v7x, 256 devices: a whole 4x4x8 slice. The times are simulated.
256 devices in a mesh: section: 4 (over x), tok: 32 (over z, y), head: 2 (over core).
Axes of the slice: x: 4, y: 4, z: 8, core: 2. Of those that a mesh axis runs over, the one named last changes fastest.
Arguments:
- group_in: bfloat16 [4, 4096, 2048], P('section', 'tok'), may hold values from -6 to 6
- w_qkv: bfloat16 [4, 3, 2048, 2048], P('section', None, 'tok', 'head'), may hold values from -0.125 to 0.125
- w_out: bfloat16 [4, 2048, 2048], P('section', 'head', 'tok'), may hold values from -0.125 to 0.125
- step_sizes: float32 [4, 4096, 4], P('section', 'tok', 'head'), may hold values from 0.05 to 1
- fast_weights: bfloat16 [4, 4, 3, 512, 512], P('section', 'head'), may hold values from -0.25 to 0.25
- momentum: bfloat16 [4, 4, 3, 512, 512], P('section', 'head'), may hold values from -48 to 48
- momentum_decay: float32 [4, 4], P('section', 'head'), may hold values from 0.5 to 0.95
- fast_rate: float32 [4, 4], P('section', 'head'), may hold values from 0.3 to 1
Outputs:
- handed: bfloat16 [4, 4096, 2048], P('section', 'tok', 'head')
- fast_next: bfloat16 [4, 4, 3, 512, 512], P('section', 'head')
All inputs are finite; a program needn't handle non-finite values.
Results may differ from a plain program's by a relative error of at most 0.015.
Values may be sent and summed in bfloat16 or wider, within the bound.
No kernel may reach another device: no remote copies, remote signals or barrier semaphores. Data moves between devices by JAX's collectives and lax.ppermute only.
A program may use at most 128 MiB of HBM per device.

v0:
```python
import jax
import jax.numpy as jnp
from jax import lax
from jax.sharding import Mesh
from jax.sharding import PartitionSpec as P

NS_ITERS = 2
TOK = ("tok_0", "tok_1")
coef_linear = 3.4445
coef_cubic = -4.775
coef_quintic = 2.0315


def gathered_by_axis(shard, axes, dim):
    if not axes:
        return shard
    nearer = lax.all_gather(shard, axes[-1], axis=dim, tiled=True)
    return gathered_by_axis(nearer, axes[:-1], dim)


def split_up(shard, dim, count):
    lengths = shard.shape
    blocks = shard.reshape(*lengths[:dim], count, lengths[dim] // count, *lengths[dim + 1 :])
    return jnp.moveaxis(blocks, dim, 0)


def sum_at_owner(shard, axis, dim):
    count = lax.axis_size(axis)
    blocks = lax.all_to_all(split_up(shard, dim, count), axis, 0, 0, tiled=True)
    return jnp.sum(blocks.astype(jnp.float32), axis=0)


def passed_along(value, axis, steps):
    count = lax.axis_size(axis)
    pairs = [(source, (source + steps) % count) for source in range(count)]
    return lax.ppermute(value, axis, pairs)


def rms_rows(values_in, epsilon):
    return values_in * lax.rsqrt(jnp.mean(values_in * values_in, axis=-1, keepdims=True) + epsilon)


def fast_grads(key_rows, value_rows, step_rates, weights):
    gate_pre = jnp.einsum(
        "thi,hij->thj", key_rows, weights[:, 0], preferred_element_type=jnp.float32
    )
    up_pre = jnp.einsum("thi,hij->thj", key_rows, weights[:, 1], preferred_element_type=jnp.float32)
    squash = jax.nn.sigmoid(gate_pre)
    hidden = (gate_pre * squash * up_pre).astype(jnp.bfloat16)
    errors = (-(step_rates[:, :, None] * value_rows.astype(jnp.float32))).astype(jnp.bfloat16)
    back_hidden = jnp.einsum(
        "thi,hij->thj", errors, weights[:, 2], preferred_element_type=jnp.float32
    )
    grad_gate = (back_hidden * up_pre * squash * (1.0 + gate_pre * (1.0 - squash))).astype(
        jnp.bfloat16
    )
    grad_up = (back_hidden * gate_pre * squash).astype(jnp.bfloat16)
    grad_first = jnp.einsum("thi,thj->hij", key_rows, grad_gate, preferred_element_type=jnp.float32)
    grad_third = jnp.einsum("thi,thj->hij", key_rows, grad_up, preferred_element_type=jnp.float32)
    grad_second = jnp.einsum("thi,thj->hij", errors, hidden, preferred_element_type=jnp.float32)
    return jnp.stack([grad_first, grad_third, grad_second], axis=1)


def newton_step(rows_in, gathered):
    gram_matrix = jnp.einsum(
        "mij,mik->mjk", gathered, gathered, preferred_element_type=jnp.float32
    ).astype(jnp.bfloat16)
    cubic_term = jnp.einsum(
        "mij,mjk->mik", rows_in, gram_matrix, preferred_element_type=jnp.float32
    )
    quintic_term = jnp.einsum(
        "mij,mjk->mik",
        cubic_term.astype(jnp.bfloat16),
        gram_matrix,
        preferred_element_type=jnp.float32,
    )
    return (
        coef_linear * rows_in.astype(jnp.float32)
        + coef_cubic * cubic_term
        + coef_quintic * quintic_term
    ).astype(jnp.bfloat16)


def apply_fast(queries, updated):
    gate_pre = jnp.einsum(
        "thi,hij->thj", queries, updated[:, 0], preferred_element_type=jnp.float32
    )
    up_pre = jnp.einsum("thi,hij->thj", queries, updated[:, 1], preferred_element_type=jnp.float32)
    hidden = (jax.nn.silu(gate_pre) * up_pre).astype(jnp.bfloat16)
    output = jnp.einsum("thj,hij->thi", hidden, updated[:, 2], preferred_element_type=jnp.float32)
    return rms_rows(output, 1e-05).astype(jnp.bfloat16)


def shards(group_in, w_qkv, w_out, step_sizes, fast_weights, momentum, momentum_decay, fast_rate):
    tokens = group_in[0]
    tok_rows = tokens.shape[0]
    local_heads = fast_weights.shape[1]
    fan_width = fast_weights.shape[3]
    hid_width = fast_weights.shape[4]
    half_width = w_qkv.shape[3]
    projected = jnp.einsum(
        "td,jde->jte",
        tokens,
        lax.all_gather(w_qkv[0], TOK, axis=1, tiled=True),
        preferred_element_type=jnp.float32,
    )
    shaped = projected.reshape(3, tok_rows, local_heads, fan_width)
    queries = rms_rows(shaped[0], 1e-06).astype(jnp.bfloat16)
    key_rows = rms_rows(shaped[1], 1e-06).astype(jnp.bfloat16)
    value_rows = shaped[2].astype(jnp.bfloat16)
    gradients = fast_grads(key_rows, value_rows, step_sizes[0], fast_weights[0])
    decay_rate = momentum_decay[0][:, None, None, None]
    summed = lax.psum(gradients.astype(jnp.bfloat16), TOK).astype(jnp.float32)
    moment = decay_rate * momentum[0].astype(jnp.float32) + summed
    norm_values = jnp.sqrt(jnp.sum(moment * moment, axis=(2, 3), keepdims=True))
    iterate = (moment / (norm_values + 1e-06)).astype(jnp.bfloat16)
    iterate = iterate.reshape(local_heads * 3, fan_width, hid_width)
    for number in range(NS_ITERS):
        iterate = newton_step(iterate, iterate)
    iterate = iterate.reshape(local_heads, 3, fan_width, hid_width)
    updated = (
        fast_weights[0].astype(jnp.float32)
        - fast_rate[0][:, None, None, None] * iterate.astype(jnp.float32)
    ).astype(jnp.bfloat16)
    mixed_heads = apply_fast(queries, updated).reshape(tok_rows, half_width)
    partial_out = jnp.dot(
        mixed_heads, gathered_by_axis(w_out[0], TOK, 1), preferred_element_type=jnp.float32
    )
    summed_out = sum_at_owner(partial_out.astype(jnp.bfloat16), "head", 1)
    share_width = summed_out.shape[1]
    own_tokens = lax.dynamic_slice_in_dim(
        tokens, lax.axis_index("head") * share_width, share_width, 1
    )
    layer_out = (own_tokens.astype(jnp.float32) + summed_out).astype(jnp.bfloat16)
    handed = passed_along(layer_out[None], "section", 1)
    return (handed, updated[None])


def solution(mesh):
    torus = Mesh(
        mesh.devices.reshape(mesh.shape["section"], 8, 4, mesh.shape["head"]),
        ("section", "tok_0", "tok_1", "head"),
    )
    return jax.shard_map(
        shards,
        mesh=torus,
        in_specs=(
            P("section", TOK, None),
            P("section", None, TOK, "head"),
            P("section", "head", TOK),
            P("section", TOK, "head"),
            P("section", "head", None, None, None),
            P("section", "head", None, None, None),
            P("section", "head"),
            P("section", "head"),
        ),
        out_specs=(P("section", TOK, "head"), P("section", "head", None, None, None)),
        check_vma=False,
    )
```

profile of v0, /device:TPU:1, one launch (start us, length us, event | category | flops | bytes accessed | tf_op | source)
XLA Modules:
  0.0 375.4 jit_solution(4437180911537350289)
XLA Ops:
  8.8 2.1 copy.71
  10.9 122.4 %all-gather.6.cloned.1.call-done = bf16[1,3,2048,1024]{3,2,1,0:T(8,128)(2,1)} async-done(((bf16[1,3,64,1024]{3,2,1,0:T(8,128)(2,1)}), bf16[1,3,2048,1024]{3,2,1,0:T(8,128)(2,1)}) %all-gather.6.cloned.1.call-update) | async-done | bytes 12582928 | tf_op jit(solution)/shard_map/all_gather | solution.py:104
  133.3 6.6 %fusion.19 = f32[3,128,1024]{1,2,0:T(8,128)S(1)} fusion(bf16[1,3,2048,1024]{3,2,1,0:T(8,128)(2,1)} %all-gather.6.cloned.1.call-done, bf16[1,128,2048]{2,1,0:T(8,128)(2,1)} %param.8), kind=kOutput, calls=%fused_computation.27 | convolution fusion | flops 1610612736 | bytes 14680064 | tf_op jit(solution)/shard_map/td,jde->jte/dot_general | solution.py:101
  143.5 2.0 pad_maximum_fusion
  145.6 10.9 %all-gather.1 = bf16[1,1024,256]{1,2,0:T(8,128)(2,1)} all-gather(bf16[1,1024,64]{1,2,0:T(8,128)(2,1)S(1)} %copy-done.6), channel_id=3, replica_groups=mesh['section'=4,'tok_0'=8,'tok_1'=4,'head'=2] {'tok_1'}, dimensions={2}, use_global_device_ids=true | all-gather | bytes 655360 | tf_op jit(solution)/shard_map/all_gather | solution.py:17
  157.7 2.0 copy.44
  159.8 157.7 %all-reduce.2.cloned.1.call-done = bf16[2,3,512,512]{3,2,0,1:T(8,128)(2,1)} async-done(((bf16[2,3,512,512]{3,2,0,1:T(8,128)(2,1)}), bf16[2,3,512,512]{3,2,0,1:T(8,128)(2,1)}) %all-reduce.2.cloned.1.call-update) | async-done | bytes 3145744 | tf_op jit(solution)/shard_map/psum | solution.py:113
  317.5 3.5 multiply_reduce_fusion
  321.0 1.3 divide_convert_fusion
  322.5 1.8 convolution_convert_fusion.1
  324.3 1.8 fusion.47
  326.1 2.2 add_convert_fusion.1
  328.4 1.8 convolution_convert_fusion
  330.2 1.8 fusion.48
  332.0 2.5 fusion.7
  334.6 5.4 %fusion.4 = bf16[2,3,512,512]{3,2,0,1:T(8,128)(2,1)S(1)} fusion(f32[2,3,512,512]{3,2,1,0:T(8,128)S(1)} %bitcast.115, f32[2]{0:T(128)S(1)} %bitcast.131, bf16[1,2,3,512,512]{4,3,2,1,0:T(8,128)(2,1)} %param.12), kind=kLoop, calls=%fused_computation.6 | loop fusion | flops 6291456 | bytes 12582920 | tf_op jit(solution)/shard_map/convert_element_type | solution.py:124
  340.0 1.7 copy-done.4
  341.6 1.1 convolution_bitcast_fusion.1
  342.7 2.6 multiply_reduce_fusion.1
  345.5 3.9 %fusion.16 = bf16[128,2048]{1,0:T(8,128)(2,1)S(1)} fusion(bf16[128,1024]{0,1:T(8,128)(2,1)S(1)} %bitcast.130, bf16[1,1024,2048]{1,2,0:T(8,128)(2,1)} %all-gather.8.cloned.1.call-done), kind=kOutput, calls=%fused_computation.21 | convolution fusion | flops 537133056 | bytes 4980736 | tf_op jit(solution)/shard_map/dot_general | solution.py:126
  349.4 8.9 %all_to_all.5 = bf16[2,128,1024]{2,1,0:T(8,128)(2,1)S(1)} all-to-all(bf16[2,128,1024]{2,1,0:T(8,128)(2,1)S(1)} %bitcast.127), channel_id=1, replica_groups=mesh['section'=4,'tok_0'=8,'tok_1'=4,'head'=2] {'head'}, dimensions={0} | all-to-all | bytes 1048576 | tf_op jit(solution)/shard_map/all_to_all | solution.py:29
  358.4 1.3 collective-permute-start
  359.7 2.8 subtract_convert_fusion
  362.5 4.7 %collective-permute-done = bf16[1,128,1024]{2,1,0:T(8,128)(2,1)S(1)} collective-permute-done((bf16[1,128,1024]{2,1,0:T(8,128)(2,1)S(1)}, bf16[1,128,1024]{2,1,0:T(8,128)(2,1)S(1)}, u32[]{:S(2)}, u32[]{:S(2)}) %collective-permute-start) | collective-permute-done | bytes 262176 | tf_op jit(solution)/shard_map/ppermute | solution.py:36
  (54 shorter events, 6.8 us)
Async XLA Ops:
  8.0 125.3 %all-gather.6.cloned.1.call-start = ((), (), s32[]{:S(2)}) async-start(), calls=%async_computation.2 | async-start | bytes 12976128 | tf_op jit(solution)/shard_map/all_gather | solution.py:104
  8.7 308.8 %all-reduce.2.cloned.1.call-start = ((), (), s32[]{:S(2)}) async-start(), calls=%async_computation.1 | async-start | bytes 6291456 | tf_op jit(solution)/shard_map/psum | solution.py:113
  140.8 0.9 copy-start.10
  143.5 2.1 copy-start.6
  145.5 172.0 %copy-start.2 = (bf16[1,2,3,512,512]{4,3,2,1,0:T(8,128)(2,1)S(1)}, bf16[1,2,3,512,512]{4,3,2,1,0:T(8,128)(2,1)}, u32[]{:S(2)}) copy-start(bf16[1,2,3,512,512]{4,3,2,1,0:T(8,128)(2,1)} %param.13) | copy-start | bytes 9437188
  145.5 172.0 %copy-start.9 = (f32[1,2]{1,0:T(1,128)S(1)}, f32[1,2]{1,0:T(1,128)}, u32[]{:S(2)}) copy-start(f32[1,2]{1,0:T(1,128)} %param.14) | copy-start | bytes 28
  145.6 199.9 %all-gather.8.cloned.1.call-start = ((), (), s32[]{:S(2)}) async-start(), calls=%async_computation.3 | async-start | bytes 4718592 | tf_op jit(solution)/shard_map/all_gather | solution.py:17
  317.5 3.5 copy-start.3
  332.0 2.5 copy-start.8
  334.5 5.4 %copy-start = (f32[6,512,512]{2,1,0:T(8,128)}, f32[6,512,512]{2,1,0:T(8,128)S(1)}, u32[]{:S(2)}) copy-start(f32[6,512,512]{2,1,0:T(8,128)S(1)} %fusion.7) | copy-start | bytes 18874372
  334.6 7.1 %copy-start.5 = (f32[128,2,512]{2,0,1:T(8,128)S(1)}, f32[128,2,512]{2,0,1:T(8,128)}, u32[]{:S(2)}) copy-start(f32[128,2,512]{2,0,1:T(8,128)} %copy.44) | copy-start | bytes 1572868
  339.9 1.7 copy-start.4
  342.7 17.0 %slice-start = ((s8[6291456]{0:T(1024)(128)(4,1)}), s8[2097152]{0:T(1024)(128)(4,1)S(1)}, s32[]{:S(2)}) async-start(s8[6291456]{0:T(1024)(128)(4,1)} %bitcast.116), calls=%async_computation.4 | async-start | bytes 4194304
  345.4 12.9 %copy-start.7 = (bf16[1,128,2048]{2,1,0:T(8,128)(2,1)S(1)}, bf16[1,128,2048]{2,1,0:T(8,128)(2,1)}, u32[]{:S(2)}) copy-start(bf16[1,128,2048]{2,1,0:T(8,128)(2,1)} %param.8) | copy-start | bytes 1572868
  345.4 14.3 %slice-start.1 = ((s8[6291456]{0:T(1024)(128)(4,1)}), s8[4194304]{0:T(1024)(128)(4,1)S(1)}, s32[]{:S(2)}) async-start(s8[6291456]{0:T(1024)(128)(4,1)} %bitcast.116), calls=%async_computation.5 | async-start | bytes 8388608
  349.3 10.4 %copy-start.1 = (bf16[1,2,3,512,512]{4,3,2,1,0:T(8,128)(2,1)S(1)}, bf16[1,2,3,512,512]{4,3,2,1,0:T(8,128)(2,1)}, u32[]{:S(2)}) copy-start(bf16[1,2,3,512,512]{4,3,2,1,0:T(8,128)(2,1)} %param.12) | copy-start | bytes 9437188
  358.4 8.8 %collective-permute-start = (bf16[1,128,1024]{2,1,0:T(8,128)(2,1)S(1)}, bf16[1,128,1024]{2,1,0:T(8,128)(2,1)S(1)}, u32[]{:S(2)}, u32[]{:S(2)}) collective-permute-start(bf16[1,128,1024]{2,1,0:T(8,128)(2,1)S(1)} %fusion.29), channel_id=1, source_target_pairs={{0,64},{64,128},{128,192},{192,0},{1,65},{65,129},{129,193},{193,1... | collective-permute-start | bytes 786440 | tf_op jit(solution)/shard_map/ppermute | solution.py:36
Sparse Core Ops, SparseCore 0:
  11.4 121.8 all-gather.5
  145.7 171.7 all-reduce.1
Sparse Core Ops, SparseCore 1:
  156.7 64.3 all-gather.7
where the time goes:
time: 376 us; the launch traced here: 375 us
  waiting for transfers between devices  286 us (76%)
  matrix products  28.7 us (8%)
  blocking collectives  19.8 us (5%)
  other arithmetic  16.4 us (4%)
  between operations  15.8 us (4%)
  local copies, waits for them, and re-layouts  7.67 us (2%)
    psum x1, waiting for transfers between devices, shards(): summed = lax.psum(gradients.astype(jnp.bfloat16), TOK).astype(jnp.float32)  158 us
    all_gather x1, waiting for transfers between devices, shards(): lax.all_gather(w_qkv[0], TOK, axis=1, tiled=True)  122 us
    all_gather x1, blocking collectives, gathered_by_axis(): nearer = lax.all_gather(shard, axes[-1], axis=dim, tiled=True)  10.9 us
    all_to_all x1, blocking collectives, sum_at_owner(): blocks = lax.all_to_all(split_up(shard, dim, count), axis, 0, 0, tiled=True)  8.89 us
    convert_element_type x2, other arithmetic, shards(): updated = (fast_weights[0].astype(jnp.float32) - fast_rate[0][:, None, No...  8.16 us
  transfers between devices with their start and end apart: 4, of which 3 were waited for; matrix products, arithmetic and copies ran while one was open for 9% of the time, Pallas kernels for 0%

commit v1 on v0

--- a/solution.py
+++ b/solution.py
@@ -110,7 +110,9 @@
     value_rows = shaped[2].astype(jnp.bfloat16)
     gradients = fast_grads(key_rows, value_rows, step_sizes[0], fast_weights[0])
     decay_rate = momentum_decay[0][:, None, None, None]
-    summed = lax.psum(gradients.astype(jnp.bfloat16), TOK).astype(jnp.float32)
+    summed = jnp.sum(lax.all_gather(gradients.astype(jnp.bfloat16), TOK), axis=0).astype(
+        jnp.float32
+    )
     moment = decay_rate * momentum[0].astype(jnp.float32) + summed
     norm_values = jnp.sqrt(jnp.sum(moment * moment, axis=(2, 3), keepdims=True))
     iterate = (moment / (norm_values + 1e-06)).astype(jnp.bfloat16)

time: 376 us -> 872 us (2.32)
  waiting for transfers between devices: 286 us -> 738 us
  other arithmetic: 16.4 us -> 50.4 us
    all_gather x0 -> x1, waiting for transfers between devices: none -> 610 us  [shards(): lax.all_gather(gradients.astype(jnp.bfloat16), TOK)]
    psum x1 -> x0, waiting for transfers between devices: 158 us -> none  [shards(): summed = lax.psum(gradients.astype(jnp.bfloat16), TOK).astype(jnp.float32)]
    reduce_sum x0 -> x1, other arithmetic: none -> 31.9 us  [shards(): jnp.sum(lax.all_gather(gradients.astype(jnp.bfloat16), TOK), axis=0)]
  transfers between devices with their start and end apart: 4 -> 4, of which waited for: 3 -> 3; matrix products, arithmetic and copies ran while one was open for 9% -> 10% of each run, Pallas kernels for 0% -> 0%
where the time goes in v1:
time: 872 us
  waiting for transfers between devices  738 us (85%)
  other arithmetic  50.4 us (6%)
  matrix products  36 us (4%)
  blocking collectives  16.2 us (2%)
  local copies, waits for them, and re-layouts  16 us (2%)
  between operations  14.1 us (2%)
    all_gather x1, waiting for transfers between devices, shards(): lax.all_gather(gradients.astype(jnp.bfloat16), TOK)  610 us
    all_gather x1, waiting for transfers between devices, shards(): lax.all_gather(w_qkv[0], TOK, axis=1, tiled=True)  122 us
    reduce_sum x1, other arithmetic, shards(): jnp.sum(lax.all_gather(gradients.astype(jnp.bfloat16), TOK), axis=0)  31.9 us
  transfers between devices with their start and end apart: 4, of which 3 were waited for; matrix products, arithmetic and copies ran while one was open for 10% of the time, Pallas kernels for 0%

profile of v1, /device:TPU:1, one launch (start us, length us, event | category | flops | bytes accessed | tf_op | source)
XLA Modules:
  0.0 871.6 jit_solution(2070891316904097039)
XLA Ops:
  7.9 2.1 copy.96
  10.0 122.4 %all-gather.9.cloned.1.call-done = bf16[1,3,2048,1024]{3,2,1,0:T(8,128)(2,1)} async-done(((bf16[1,3,64,1024]{3,2,1,0:T(8,128)(2,1)}), bf16[1,3,2048,1024]{3,2,1,0:T(8,128)(2,1)}) %all-gather.9.cloned.1.call-update) | async-done | bytes 12582928 | tf_op jit(solution)/shard_map/all_gather | solution.py:104
  132.5 6.6 fusion.23
  143.1 2.1 copy.57
  145.2 10.8 %all-gather.1 = bf16[1,1024,256]{1,2,0:T(8,128)(2,1)} all-gather(bf16[1,1024,64]{1,2,0:T(8,128)(2,1)S(1)} %copy-done.7), channel_id=3, replica_groups=mesh['section'=4,'tok_0'=8,'tok_1'=4,'head'=2] {'tok_1'}, dimensions={2}, use_global_device_ids=true | all-gather | bytes 655360 | tf_op jit(solution)/shard_map/all_gather | solution.py:17
  157.1 3.8 copy.52
  161.9 609.6 %all-gather.7.cloned.1.call-done = bf16[32,2,3,512,512]{4,3,2,1,0:T(8,128)(2,1)} async-done(((bf16[1,2,3,512,512]{4,3,2,1,0:T(8,128)(2,1)}), bf16[32,2,3,512,512]{4,3,2,1,0:T(8,128)(2,1)}) %all-gather.7.cloned.1.call-update) | async-done | bytes 100663312 | tf_op jit(solution)/shard_map/all_gather | solution.py:113
  771.6 31.9 %reduce_sum.60 = bf16[2,3,512,512]{3,2,1,0:T(8,128)(2,1)S(1)} reduce(bf16[32,2,3,512,512]{4,3,2,1,0:T(8,128)(2,1)} %all-gather.7.cloned.1.call-done, bf16[]{:T(256)} %constant.30.clone.1), dimensions={0}, to_apply=%region_1.0 | reduce | flops 48758784 | bytes 103809024 | tf_op jit(solution)/shard_map/reduce_sum | solution.py:113
  804.3 3.4 copy.59
  807.7 1.5 fusion.4
  809.4 6.5 fusion.6
  815.8 1.8 convolution_convert_fusion.1
  817.7 4.5 fusion.51
  822.1 6.8 add_convert_fusion.1
  829.0 1.8 convolution_convert_fusion
  830.8 2.0 fusion.52
  832.9 2.2 fusion.11
  835.1 5.4 fusion.8
  840.5 1.7 copy-done.4
  843.4 2.6 multiply_reduce_fusion
  846.1 3.9 fusion.20
  850.0 5.5 all_to_all.5
  856.9 2.8 subtract_convert_fusion
  859.7 4.7 collective-permute-done
  (65 shorter events, 11.4 us)
Async XLA Ops:
  7.2 125.3 %all-gather.9.cloned.1.call-start = ((), (), s32[]{:S(2)}) async-start(), calls=%async_computation.2 | async-start | bytes 12976128 | tf_op jit(solution)/shard_map/all_gather | solution.py:104
  7.9 763.7 %all-gather.7.cloned.1.call-start = ((), (), s32[]{:S(2)}) async-start(), calls=%async_computation.1 | async-start | bytes 103809024 | tf_op jit(solution)/shard_map/all_gather | solution.py:113
  140.0 0.9 copy-start.10
  143.1 2.1 copy-start.7
  145.1 10.9 %copy-start.11 = (f32[1,2]{1,0:T(1,128)S(1)}, f32[1,2]{1,0:T(1,128)}, u32[]{:S(2)}) copy-start(f32[1,2]{1,0:T(1,128)} %param.14) | copy-start | bytes 28
  145.1 11.1 %copy-start.2 = (bf16[1,2,3,512,512]{4,3,2,1,0:T(8,128)(2,1)S(1)}, bf16[1,2,3,512,512]{4,3,2,1,0:T(8,128)(2,1)}, u32[]{:S(2)}) copy-start(bf16[1,2,3,512,512]{4,3,2,1,0:T(8,128)(2,1)} %param.13) | copy-start | bytes 9437188
  145.2 700.9 %all-gather.11.cloned.1.call-start = ((), (), s32[]{:S(2)}) async-start(), calls=%async_computation.3 | async-start | bytes 4718592 | tf_op jit(solution)/shard_map/all_gather | solution.py:17
  157.1 3.8 copy-start.5
  804.3 3.4 copy-start.3
  832.9 2.3 copy-start.9
  835.1 5.4 copy-start
  835.1 7.1 copy-start.6
  840.5 1.7 copy-start.4
  843.4 13.5 %slice-start = ((s8[6291456]{0:T(1024)(128)(4,1)}), s8[2097152]{0:T(1024)(128)(4,1)S(1)}, s32[]{:S(2)}) async-start(s8[6291456]{0:T(1024)(128)(4,1)} %bitcast.126), calls=%async_computation.4 | async-start | bytes 4194304
  846.0 9.5 %copy-start.8 = (bf16[1,128,2048]{2,1,0:T(8,128)(2,1)S(1)}, bf16[1,128,2048]{2,1,0:T(8,128)(2,1)}, u32[]{:S(2)}) copy-start(bf16[1,128,2048]{2,1,0:T(8,128)(2,1)} %param.8) | copy-start | bytes 1572868
  846.0 10.8 %slice-start.1 = ((s8[6291456]{0:T(1024)(128)(4,1)}), s8[4194304]{0:T(1024)(128)(4,1)S(1)}, s32[]{:S(2)}) async-start(s8[6291456]{0:T(1024)(128)(4,1)} %bitcast.126), calls=%async_computation.5 | async-start | bytes 8388608
  849.9 7.0 copy-start.1
  855.6 8.8 %collective-permute-start = (bf16[1,128,1024]{2,1,0:T(8,128)(2,1)S(1)}, bf16[1,128,1024]{2,1,0:T(8,128)(2,1)S(1)}, u32[]{:S(2)}, u32[]{:S(2)}) collective-permute-start(bf16[1,128,1024]{2,1,0:T(8,128)(2,1)S(1)} %fusion.33), channel_id=1, source_target_pairs={{0,64},{64,128},{128,192},{192,0},{1,65},{65,129},{129,193},{193,1... | collective-permute-start | bytes 786440 | tf_op jit(solution)/shard_map/ppermute | solution.py:36
Sparse Core Ops, SparseCore 0:
  10.6 121.8 all-gather.8
  145.3 626.2 all-gather.6
  773.4 52.3 all-gather.10
